TPU v7x, 128 devices: a whole 4x4x4 slice. The times are simulated.
128 devices in a mesh: replica: 8 (over z, core), tp: 16 (over y, x).
Axes of the slice: x: 4, y: 4, z: 4, core: 2. Of those that a mesh axis runs over, the one named last changes fastest.
Arguments:
- hidden: bfloat16 [1024, 8192], P(('replica', 'tp')), may hold values from -64 to 64
- head: bfloat16 [152064, 8192], P(('replica', 'tp'))
- token_ids: int32 [1024], replicated, may hold values from 0 to 152063
Outputs:
- logprob: float32 [1024], P(('replica', 'tp'))
All inputs are finite; a program needn't handle non-finite values.
Results may differ from a plain program's by a relative error of at most 0.0003.
Values may be sent and summed in bfloat16 or wider, within the bound.
A program may use at most 128 MiB of HBM per device.

v0:
```python
import jax
import jax.numpy as jnp
from jax import lax
from jax.sharding import PartitionSpec as P


def in_one_piece(arrays, axis, split_dim, concat_dim, along):
    widths = [a.shape[along] for a in arrays]
    both = jnp.concatenate(arrays, axis=along)
    out = lax.all_to_all(both, axis, split_axis=split_dim, concat_axis=concat_dim, tiled=True)
    return tuple(jnp.split(out, [sum(widths[:k]) for k in range(1, len(widths))], axis=along))


def shards(hidden, head, token_ids):
    device_count = lax.axis_size("replica") * lax.axis_size("tp")
    per_device = hidden.shape[0]
    local_vocab = head.shape[0]
    position = lax.axis_index(("replica", "tp"))
    columns = position * local_vocab + jnp.arange(local_vocab, dtype=jnp.int32)
    gathered = lax.all_gather(hidden, ("replica", "tp"), axis=0, tiled=True)
    logits = lax.dot_general(
        gathered, head, (((1,), (1,)), ((), ())), preferred_element_type=jnp.float32
    )
    row_top = jnp.max(logits, axis=1)
    row_total = jnp.sum(jnp.exp(logits - row_top[:, None]), axis=1)
    row_picked = jnp.sum(jnp.where(columns[None, :] == token_ids[:, None], logits, 0.0), axis=1)
    stats = (row_top, row_total, row_picked)
    row_top, row_total, row_picked = stats
    shaped = (
        row_top.reshape(device_count, per_device),
        row_total.reshape(device_count, per_device),
        row_picked.reshape(device_count, per_device),
    )
    arrived = in_one_piece((shaped[0], shaped[1], shaped[2]), ("replica", "tp"), 0, 0, 1)
    final_top = jnp.max(arrived[0], axis=0)
    final_total = jnp.sum(arrived[1] * jnp.exp(arrived[0] - final_top[None, :]), axis=0)
    final_picked = jnp.sum(arrived[2], axis=0)
    return final_picked - final_top - jnp.log(final_total)


def solution(mesh):
    in_specs = (P(("replica", "tp"), None), P(("replica", "tp"), None), P())
    out_specs = P(("replica", "tp"))
    return jax.shard_map(shards, mesh=mesh, in_specs=in_specs, out_specs=out_specs, check_vma=False)
```

profile of v0, /device:TPU:1, one launch (start us, length us, event | category | flops | bytes accessed | tf_op | source)
XLA Modules:
  0.0 149.2 jit_solution(16097349257414862518)
XLA Ops:
  6.5 0.0 all-gather.2.cloned.1.call-start
  6.5 0.7 all-gather.2.cloned.1.call-update
  7.3 0.0 copy-start
  7.3 86.8 %all-gather.2.cloned.1.call-done = bf16[1024,8192]{1,0:T(8,128)(2,1)} async-done(((bf16[8,8192]{1,0:T(8,128)(2,1)}), bf16[1024,8192]{1,0:T(8,128)(2,1)}) %all-gather.2.cloned.1.call-update) | async-done | bytes 16777232 | tf_op jit(solution)/shard_map/all_gather | solution.py:20
  94.1 27.3 %fusion.1 = (f32[1024]{0:T(1024)S(1)}, f32[1024,1188]{0,1:T(8,128)}) fusion(bf16[1024,8192]{1,0:T(8,128)(2,1)} %all-gather.2.cloned.1.call-done, bf16[1188,8192]{1,0:T(8,128)(2,1)} %param.4), kind=kOutput, calls=%fused_computation.9 | convolution fusion | flops 19932549120 | bytes 41111552 | tf_op jit(solution)/shard_map/dot_general | solution.py:21
  121.4 0.1 reshape.18
  121.5 0.0 copy-done
  121.5 3.1 %exponential_reduce_fusion = (f32[1024]{0:T(1024)S(1)}, f32[1024]{0:T(1024)S(1)}) fusion(f32[1024,1188]{0,1:T(8,128)} %get-tuple-element.10, f32[1024]{0:T(1024)S(1)} %get-tuple-element.9, s32[1024]{0:T(1024)S(1)} %copy-done, s32[1188]{0:T(1024)S(1)} %iota_add_fusion), kind=kLoop, calls=%fused_computation.1 | loop fusion | flops 6080512 | bytes 4887184 | tf_op jit(solution)/shard_map/reduce_sum | solution.py:25
  124.6 0.1 reshape.19
  124.7 0.1 reshape.20
  124.8 0.1 pad_maximum_fusion
  124.9 16.8 %all_to_all.12 = f32[128,1,24]{2,1,0:T(1,128)S(1)} all-to-all(f32[128,1,24]{2,1,0:T(1,128)S(1)} %bitcast.8), channel_id=1, replica_groups=mesh['replica'=8,'tp'=16] {'replica','tp'}, dimensions={0} | all-to-all | bytes 24576 | tf_op jit(solution)/shard_map/all_to_all | solution.py:10
  141.8 0.1 slice_reduce_fusion
  141.9 0.5 log_subtract_fusion
  (2 shorter events, 0.0 us)
Async XLA Ops:
  6.5 87.6 %all-gather.2.cloned.1.call-start = ((), (), s32[]{:S(2)}) async-start(), calls=%async_computation.1 | async-start | bytes 16908288 | tf_op jit(solution)/shard_map/all_gather | solution.py:20
  7.3 114.2 %copy-start = (s32[1024]{0:T(1024)S(1)}, s32[1024]{0:T(1024)}, u32[]{:S(2)}) copy-start(s32[1024]{0:T(1024)} %param.5) | copy-start | bytes 12292
Sparse Core Ops, SparseCore 0:
  10.5 83.5 all-gather.1
where the time goes:
time: 149 us
  waiting for transfers between devices  87.5 us (59%)
  matrix products  27.3 us (18%)
  blocking collectives  16.8 us (11%)
  between operations  13.5 us (9%)
  other arithmetic  3.93 us (3%)
    all_gather x1, waiting for transfers between devices, shards(): gathered = lax.all_gather(hidden, ('replica', 'tp'), axis=0, tiled=True)  86.8 us
    dot_general x1, matrix products, shards(): lax.dot_general(gathered, head, (((1,), (1,)), ((), ())), preferred_eleme...  27.3 us
    all_to_all x1, blocking collectives, in_one_piece(): lax.all_to_all(both, axis, split_axis=split_dim, concat_axis=concat_dim,...  16.8 us
    reduce_sum x1, other arithmetic, shards(): row_total = jnp.sum(jnp.exp(logits - row_top[:, None]), axis=1)  3.15 us
  transfers between devices with their start and end apart: 1, of which 1 were waited for; matrix products, arithmetic and copies ran while one was open for 0% of the time, Pallas kernels for 0%

commit v1 on v0

v1 whole, which is shorter than its diff:
```python
import functools

import jax
import jax.numpy as jnp
from jax import lax
from jax.experimental import pallas as pl
from jax.experimental.pallas import tpu as pltpu
from jax.sharding import PartitionSpec as P

MESH = pl.DeviceIdType.MESH
ROTATIONS = ((2, 1, 0), (1, 0, 2), (0, 2, 1))
UNIT = 256
WIDTHS = (11, 11, 10)
STAGE = 2
STAGES = 5
FIRST = (0, 11, 22)
ALL = (0, 4)


def at(rotation, e1, e2, e3):
    where = [None, None, None]
    for axis, e in zip(ROTATIONS[rotation], (e1, e2, e3)):
        where[axis] = pl.ds(e[0], e[1]) if isinstance(e, tuple) else e
    return tuple(where)


def kernel(hidden, head, ids, out, blocks, weights, logits, rolled, chip, chip_in, plane, plane_in,
           head_sem, own_sem, send_sem, recv_sem, loop_send, loop_recv):
    replica, tp = lax.axis_index("replica"), lax.axis_index("tp")
    z, core = replica // 2, lax.rem(replica, 2)
    y, x = tp // 4, lax.rem(tp, 4)
    vocab, depth = head.shape

    def device(dz, dy, dx, other_core):
        c = 1 - core if other_core else core
        return (lax.rem(z + dz, 4) * 2 + c, lax.rem(y + dy, 4) * 4 + lax.rem(x + dx, 4))

    def neighbour(axis, step):
        move = [0, 0, 0]
        move[axis] = step % 4
        return device(*move, False)

    sibling = device(0, 0, 0, True)

    own = pltpu.make_async_copy(hidden, blocks.at[0, 0, 0, 0], own_sem)
    own.start()
    loads = []
    for k in range(4):
        part = pl.ds(k * depth // 4, depth // 4)
        loads.append(pltpu.make_async_copy(head.at[:, part], weights.at[:, part], head_sem.at[k]))
        loads[-1].start()

    barrier = pltpu.get_barrier_semaphore()
    for axis in range(3):
        for step in (1, -1):
            pl.semaphore_signal(barrier, inc=1, device_id=neighbour(axis, step), device_id_type=MESH)
    pl.semaphore_signal(barrier, inc=1, device_id=sibling, device_id_type=MESH)
    pl.semaphore_wait(barrier, 7)
    own.wait()

    used = [0]
    started = []

    def copy(src, dst, target):
        k = used[0]
        used[0] += 1
        c = pltpu.make_async_remote_copy(
            src_ref=src, dst_ref=dst, send_sem=send_sem.at[k], recv_sem=recv_sem.at[k],
            device_id=target, device_id_type=MESH)
        c.start()
        started.append(c)
        return c

    def columns(r, first, count):
        return pl.ds((FIRST[r] + first) * UNIT, count * UNIT)

    def hop(r, which, step, src, dst, cols):
        return copy(blocks.at[(0,) + at(r, *src) + (slice(None), cols)],
                    blocks.at[(0,) + at(r, *dst) + (slice(None), cols)],
                    neighbour(ROTATIONS[r][which], step))

    def share(r, where, cols):
        return copy(blocks.at[(0,) + at(r, *where) + (slice(None), cols)],
                    blocks.at[(1,) + at(r, *where) + (slice(None), cols)], sibling)

    full = [columns(r, 0, WIDTHS[r]) for r in range(3)]
    RS = range(3)
    one_up = [hop(r, 0, 1, (0, 0, 0), (3, 0, 0), full[r]) for r in RS]
    one_down = [hop(r, 0, -1, (0, 0, 0), (1, 0, 0), full[r]) for r in RS]

    def second(r, e1):
        return (hop(r, 1, 1, (e1, 0, 0), (e1, 3, 0), full[r]), hop(r, 1, -1, (e1, 0, 0), (e1, 1, 0), full[r]))

    two = [[None] * 4 for _ in RS]
    for r in RS:
        two[r][0] = second(r, 0)

    logits[...] = jnp.zeros_like(logits)
    logits[pl.ds(vocab, 4), :] = jnp.full((4, logits.shape[1]), -3.0e38, jnp.float32)
    lane = lax.broadcasted_iota(jnp.int32, (8, 128), 1)
    turned = pltpu.roll(ids[...], lax.rem(128 - y * 32, 128), 1)
    near = pltpu.roll(turned, lax.rem(128 - x * 8, 128), 1)
    far = pltpu.roll(turned, lax.rem(160 - x * 8, 128), 1)
    turned = jnp.where(lax.rem(lane, 32) + x * 8 < 32, near, far) - (replica * 16 + tp) * vocab
    rolled[...] = jnp.where((turned >= 0) & (turned < vocab), turned, -1)

    one_far = []
    for r in RS:
        half = (WIDTHS[r] + 1) // 2
        one_up[r].wait_recv()
        a = hop(r, 0, 1, (3, 0, 0), (2, 0, 0), columns(r, 0, half))
        two[r][3] = second(r, 3)
        one_down[r].wait_recv()
        b = hop(r, 0, -1, (1, 0, 0), (2, 0, 0), columns(r, half, WIDTHS[r] - half))
        two[r][1] = second(r, 1)
        one_far.append((a, b))

    three = []
    two_far = [[None] * 4 for _ in RS]
    for r in RS:
        for c in one_far[r]:
            c.wait_recv()
        two[r][2] = second(r, 2)
        three.append((hop(r, 2, 1, (ALL, 0, 0), (ALL, 0, 3), full[r]), hop(r, 2, -1, (ALL, 0, 0), (ALL, 0, 1), full[r])))

    def onward(r, e1):
        up, down = two[r][e1]
        up.wait_recv()
        down.wait_recv()
        if e1 < 2:
            two_far[r][e1] = hop(r, 1, 1, (e1, 3, 0), (e1, 2, 0), full[r])
        else:
            two_far[r][e1] = hop(r, 1, -1, (e1, 1, 0), (e1, 2, 0), full[r])

    for e1 in (0, 1, 3, 2):
        for r in RS:
            onward(r, e1)

    REST = (1, 3)

    def loop_cols(r, s):
        return pl.ds(pl.multiple_of((FIRST[r] + s * STAGE) * UNIT, UNIT), STAGE * UNIT)

    def loop_copy(s, r, kind):
        cols = loop_cols(r, s)
        src, dst, which, step = (
            ((ALL, REST, 0), (ALL, REST, 3), 2, 1),
            ((ALL, REST, 0), (ALL, REST, 1), 2, -1),
            (((0, 2), REST, 3), ((0, 2), REST, 2), 2, 1),
            (((2, 2), REST, 1), ((2, 2), REST, 2), 2, -1),
            ((ALL, REST, (1, 3)), (ALL, REST, (1, 3)), None, None),
        )[kind]
        target = sibling if which is None else neighbour(ROTATIONS[r][which], step)
        return pltpu.make_async_remote_copy(
            src_ref=blocks.at[(0,) + at(r, *src) + (slice(None), cols)],
            dst_ref=blocks.at[(1 if which is None else 0,) + at(r, *dst) + (slice(None), cols)],
            send_sem=loop_send.at[s, r * 5 + kind], recv_sem=loop_recv.at[s, r * 5 + kind],
            device_id=target, device_id_type=MESH)

    shares = []
    for r in RS:
        for c in two_far[r]:
            c.wait_recv()
        for s in range(1):
            loop_copy(s, r, 0).start()
            loop_copy(s, r, 1).start()
        shares.append(share(r, (ALL, ALL, 0), full[r]))

    three_far = []
    for r in RS:
        three[r][0].wait_recv()
        a = hop(r, 2, 1, ((0, 2), 0, 3), ((0, 2), 0, 2), full[r])
        three[r][1].wait_recv()
        b = hop(r, 2, -1, ((2, 2), 0, 1), ((2, 2), 0, 2), full[r])
        three_far.append((a, b))
        loop_copy(1, r, 0).start()
        loop_copy(1, r, 1).start()

    tail = []
    for r in (0, 1):
        cols = columns(r, STAGE * STAGES, 1)
        tail.append((hop(r, 2, 1, (ALL, REST, 0), (ALL, REST, 3), cols), hop(r, 2, -1, (ALL, REST, 0), (ALL, REST, 1), cols)))
    for r in RS:
        for c in three_far[r]:
            c.wait_recv()
        shares.append(share(r, (ALL, 0, (1, 3)), full[r]))
    for c in loads:
        c.wait()

    half_lanes = logits.shape[1] // 2

    def multiply(side, cols):
        a = jnp.concatenate([weights[:, c] for c in cols], axis=1)
        b = jnp.concatenate([blocks[side, :, :, :, :, c].reshape(half_lanes, c.size) for c in cols], axis=1)
        product = lax.dot_general(a, b, (((1,), (1,)), ((), ())), preferred_element_type=jnp.float32)
        where = (pl.ds(0, vocab), pl.ds(side * half_lanes, half_lanes))
        logits[where] = logits[where] + product

    def arrive(s):
        for r in RS:
            loop_copy(s, r, 0).wait_recv()
            loop_copy(s, r, 2).start()
            loop_copy(s, r, 1).wait_recv()
            loop_copy(s, r, 3).start()

    def finish(s):
        for r in RS:
            loop_copy(s, r, 2).wait_recv()
            loop_copy(s, r, 3).wait_recv()
            loop_copy(s, r, 4).start()

    def stage_cols(s):
        return [loop_cols(r, s) for r in RS]

    def queue(s):
        for r in RS:
            loop_copy(s, r, 0).start()
            loop_copy(s, r, 1).start()

    arrive(0)
    queue(2)
    finish(0)
    multiply(0, stage_cols(0))
    for c in shares:
        c.wait_recv()

    def stage(s, _):
        arrive(s)

        @pl.when(s + 2 < STAGES)
        def _():
            queue(s + 2)

        for r in RS:
            loop_copy(s - 1, r, 4).wait_recv()
        multiply(1, stage_cols(s - 1))
        finish(s)
        multiply(0, stage_cols(s))
        return 0

    lax.fori_loop(1, STAGES, stage, 0)

    tail_cols = [columns(r, STAGE * STAGES, 1) for r in (0, 1)]
    tail_far = []
    for r in (0, 1):
        tail[r][0].wait_recv()
        a = hop(r, 2, 1, ((0, 2), REST, 3), ((0, 2), REST, 2), tail_cols[r])
        tail[r][1].wait_recv()
        b = hop(r, 2, -1, ((2, 2), REST, 1), ((2, 2), REST, 2), tail_cols[r])
        tail_far.append((a, b))
    for r in RS:
        loop_copy(STAGES - 1, r, 4).wait_recv()
    multiply(1, stage_cols(STAGES - 1))
    tail_share = []
    for r in (0, 1):
        for c in tail_far[r]:
            c.wait_recv()
        tail_share.append(share(r, (ALL, REST, (1, 3)), tail_cols[r]))
    multiply(0, tail_cols)
    for c in tail_share:
        c.wait_recv()
    multiply(1, tail_cols)

    lanes = logits.shape[1]
    rows = 32
    count = logits.shape[0] // rows
    left = logits.shape[0] - rows * count

    def groups(value):
        return [value[8 * k:8 * k + 8, :] for k in range(value.shape[0] // 8)]

    def top_step(i, top):
        for v in groups(logits[pl.ds(pl.multiple_of(i * rows, rows), rows), :]):
            top = jnp.maximum(top, v)
        return top

    top = lax.fori_loop(0, count, top_step, logits[pl.ds(rows * count, left), :])
    top = jnp.max(top, axis=0, keepdims=True)

    order = [(c, dz) for c in range(2) for dz in range(4)]
    wanted = jnp.concatenate(
        [rolled[pl.ds(lax.rem(z + dz, 4) * 2 + (1 - core if c else core), 1), :] for c, dz in order], axis=1)
    row = lax.broadcasted_iota(jnp.int32, (8, lanes), 0)
    offset = jnp.broadcast_to(wanted, (8, lanes)) - row

    def add(v, first, total, picked):
        total = total + jnp.exp(v - top)
        picked = picked + jnp.where(offset == first, v, 0.0)
        return total, picked

    def sum_step(i, carry):
        total, picked = carry
        for k, v in enumerate(groups(logits[pl.ds(pl.multiple_of(i * rows, rows), rows), :])):
            total, picked = add(v, i * rows + 8 * k, total, picked)
        return total, picked

    zero = jnp.zeros((8, lanes), jnp.float32)
    total, picked = lax.fori_loop(0, count, sum_step, (zero, zero))
    total, picked = add(logits[pl.ds(rows * count, left), :], rows * count, total, picked)
    total = jnp.sum(total, axis=0, keepdims=True)
    picked = jnp.sum(picked, axis=0, keepdims=True)

    for k in range(8):
        part = slice(128 * k, 128 * k + 128)
        chip[k, 0:1, :] = top[:, part]
        chip[k, 1:2, :] = total[:, part]
        chip[k, 2:3, :] = picked[:, part]
    ups = []
    for k, (c, dz) in enumerate(order):
        if k:
            ups.append(copy(chip.at[k], chip_in.at[c * 4 + (-dz) % 4], device(dz, 0, 0, c)))
    for c in ups:
        c.wait_recv()

    def merge(parts):
        best = functools.reduce(jnp.maximum, [p[0] for p in parts])
        total = sum(p[1] * jnp.exp(p[0] - best) for p in parts)
        return best, total, sum(p[2] for p in parts)

    def three_rows(ref, *at):
        return tuple(ref[at + (pl.ds(k, 1), slice(None))] for k in range(3))

    best, total, picked = merge([three_rows(chip, 0)] + [three_rows(chip_in, k) for k in range(1, 8)])
    plane[0:1, :] = best
    plane[1:2, :] = total
    plane[2:3, :] = picked
    across = []
    for dy in range(4):
        for dx in range(4):
            if dy or dx:
                across.append(copy(plane, plane_in.at[(-dy) % 4 * 4 + (-dx) % 4], device(0, dy, dx, False)))
    for c in across:
        c.wait_recv()
    group = lax.broadcasted_iota(jnp.int32, (1, 128), 1) // 8
    for sy in range(4):
        for sx in range(4):
            if sy or sx:
                mine = group == (-sy) % 4 * 4 + (-sx) % 4
                b, t, p = three_rows(plane_in, sy * 4 + sx)
                best, total, picked = jnp.where(mine, b, best), jnp.where(mine, t, total), jnp.where(mine, p, picked)
    final = best
    for shift in (8, 16, 32, 64):
        final = jnp.maximum(final, pltpu.roll(final, shift, 1))
    total = total * jnp.exp(best - final)
    for shift in (8, 16, 32, 64):
        total = total + pltpu.roll(total, shift, 1)
        picked = picked + pltpu.roll(picked, shift, 1)
    out[...] = picked - final - jnp.log(total)

    for c in started:
        c.wait_send()

    def drain(s, _):
        for r in RS:
            for kind in range(5):
                loop_copy(s, r, kind).wait_send()
        return 0

    lax.fori_loop(0, STAGES, drain, 0)


COPIES = 150


def shards(hidden, head, token_ids):
    vocab, depth = head.shape
    lanes = token_ids.shape[0]
    out = pl.pallas_call(
        kernel,
        out_shape=jax.ShapeDtypeStruct((1, 128), jnp.float32),
        in_specs=[pl.BlockSpec(memory_space=pl.ANY), pl.BlockSpec(memory_space=pl.ANY),
                  pl.BlockSpec(memory_space=pltpu.VMEM)],
        out_specs=pl.BlockSpec(memory_space=pltpu.VMEM),
        scratch_shapes=[
            pltpu.VMEM((2, 4, 4, 4, 8, depth), jnp.bfloat16),
            pltpu.VMEM((vocab, depth), jnp.bfloat16),
            pltpu.VMEM((vocab + 4, lanes), jnp.float32),
            pltpu.VMEM((8, 128), jnp.int32),
            pltpu.VMEM((8, 8, 128), jnp.float32),
            pltpu.VMEM((8, 8, 128), jnp.float32),
            pltpu.VMEM((8, 128), jnp.float32),
            pltpu.VMEM((16, 8, 128), jnp.float32),
            pltpu.SemaphoreType.DMA((4,)),
            pltpu.SemaphoreType.DMA,
            pltpu.SemaphoreType.DMA((COPIES,)),
            pltpu.SemaphoreType.DMA((COPIES,)),
            pltpu.SemaphoreType.DMA((STAGES, 15)),
            pltpu.SemaphoreType.DMA((STAGES, 15)),
        ],
        compiler_params=pltpu.CompilerParams(
            collective_id=0, has_side_effects=True, vmem_limit_bytes=60 * 1024 * 1024),
        name="logprob",
    )(hidden, head, token_ids.reshape(8, 128))
    return out[0, :8]


def solution(mesh):
    in_specs = (P(("replica", "tp"), None), P(("replica", "tp"), None), P())
    out_specs = P(("replica", "tp"))
    return jax.shard_map(shards, mesh=mesh, in_specs=in_specs, out_specs=out_specs, check_vma=False)
```

time: 149 us -> 86.7 us (0.58)
  waiting for transfers between devices: 87.5 us -> 0 us
  Pallas kernels: 0 us -> 85.3 us
  matrix products: 27.3 us -> 0 us
  blocking collectives: 16.8 us -> 0 us
  between operations: 13.5 us -> 0.01 us
  other arithmetic: 3.93 us -> 0 us
    all_gather x1 -> x0, waiting for transfers between devices: 86.8 us -> none  [shards(): gathered = lax.all_gather(hidden, ('replica', 'tp'), axis=0, tiled=True)]
    pallas_call x0 -> x1, Pallas kernels: none -> 85.3 us  [shards(): pl.pallas_call(kernel, out_shape=jax.ShapeDtypeStruct((1, 128), jnp.float...]
    dot_general x1 -> x0, matrix products: 27.3 us -> none  [shards(): lax.dot_general(gathered, head, (((1,), (1,)), ((), ())), preferred_eleme...]
    all_to_all x1 -> x0, blocking collectives: 16.8 us -> none  [in_one_piece(): lax.all_to_all(both, axis, split_axis=split_dim, concat_axis=concat_dim,...]
    reduce_sum x2 -> x0, other arithmetic: 3.27 us -> none  [the longest x1 3.15 us: shards(): row_total = jnp.sum(jnp.exp(logits - row_top[:, None]), axis=1)]
  transfers between devices with their start and end apart: 1 -> 0, of which waited for: 1 -> 0; matrix products, arithmetic and copies ran while one was open for 0% -> 0% of each run, Pallas kernels for 0% -> 0%
where the time goes in v1:
time: 86.7 us; the launch traced here: 86.5 us
  Pallas kernels  85.3 us (98%)
  local copies, waits for them, and re-layouts  1.19 us (1%)
    pallas_call x1, Pallas kernels, shards(): pl.pallas_call(kernel, out_shape=jax.ShapeDtypeStruct((1, 128), jnp.float...  85.3 us

profile of v1, /device:TPU:1, one launch (start us, length us, event | category | flops | bytes accessed | tf_op | source)
XLA Modules:
  0.0 86.5 jit_solution(16173892816744903631)
XLA Ops:
  0.0 85.3 %logprob.1 = f32[1,128]{1,0:T(1,128)} custom-call(bf16[8,8192]{1,0:T(8,128)(2,1)} %hidden.1, bf16[1188,8192]{1,0:T(8,128)(2,1)} %head.1, s32[8,128]{1,0:T(8,128)} %bitcast.3), custom_call_target="tpu_custom_call" | custom-call | tf_op jit(solution)/shard_map/logprob/pallas_call | solution.py:368
  85.3 1.2 %slice_bitcast_fusion = f32[8]{0:T(128)} fusion(f32[1,128]{1,0:T(1,128)} %logprob.1), kind=kLoop, calls=%fused_computation | loop fusion | bytes 64 | tf_op jit(solution)/shard_map/squeeze | solution.py:394

commit v2 on v0

v2 whole, which is shorter than its diff:
```python
import functools

import jax
import jax.numpy as jnp
from jax import lax
from jax.experimental import pallas as pl
from jax.experimental.pallas import tpu as pltpu
from jax.sharding import PartitionSpec as P

MESH = pl.DeviceIdType.MESH
ROTATIONS = ((2, 1, 0), (1, 0, 2), (0, 2, 1))
UNIT = 256
FIRST = (0, 11, 22)
TOTAL = (11, 11, 10)
STAGES = ((1, 1, 1), (1, 1, 1), (2, 2, 2), (2, 2, 2), (2, 2, 2), (2, 2, 2), (1, 1, 0))
WHOLE = (0, 1, 6)
PASSED = (3, 4, 5, 6)
FINAL = (3, 3)
ORDER = (
    "S0", "rest", "S5", "load", "S4", "S2", "T0", "G5", "G4", "S6", "T2", "A0",
    "S3", "T4", "M0", "G6", "A2", "G3", "T5", "A4", "N0", "S1", "F2", "T3",
    "M2", "A5", "N2", "T6", "T1", "F4", "M4", "N4", "F5", "A3", "M5", "A6",
    "N5", "M6", "A1", "N6", "M1", "F3", "M3", "N1", "N3",
)
START = tuple(tuple(FIRST[r] + sum(st[r] for st in STAGES[:k]) for r in range(3)) for k in range(len(STAGES)))
ALL, NEAR = (0, 4), (0, 3)
KINDS = 6
SECOND, PASS, DIRECT, FORWARD, SHARE, SHARE_FAR = range(KINDS)
LATE = KINDS * len(STAGES)
ONE, ONE_REST, CHIP, PLANE = range(LATE, LATE + 4)


def at(rotation, e1, e2, e3):
    where = [None, None, None]
    for axis, e in zip(ROTATIONS[rotation], (e1, e2, e3)):
        where[axis] = pl.ds(e[0], e[1]) if isinstance(e, tuple) else e
    return tuple(where)


def region(count):
    for units in range(32, 0, -1):
        if count % units:
            continue
        for c in (1, 2):
            for i in range(1, 5):
                for j in range(1, 5):
                    for k in range(1, 5):
                        if c * i * j * k * units == count:
                            return (pl.ds(0, c), pl.ds(0, i), pl.ds(0, j), pl.ds(0, k), slice(None), pl.ds(0, units * UNIT))
    raise ValueError(count)


def kernel(hidden, head, token_ids, out, blocks, weights, logits, ids, rolled, chip, chip_in, plane, plane_in,
           head_sem, own_sem, ids_sem, send_sem, recv_sem):
    replica, tp = lax.axis_index("replica"), lax.axis_index("tp")
    z, core = replica // 2, lax.rem(replica, 2)
    y, x = tp // 4, lax.rem(tp, 4)
    vocab, depth = head.shape
    RS = range(3)

    def device(dz, dy, dx, other_core):
        c = 1 - core if other_core else core
        return (lax.rem(z + dz, 4) * 2 + c, lax.rem(y + dy, 4) * 4 + lax.rem(x + dx, 4))

    def neighbour(axis, step):
        move = [0, 0, 0]
        move[axis] = step % 4
        return device(*move, False)

    sibling = device(0, 0, 0, True)

    own = pltpu.make_async_copy(hidden, blocks.at[0, 1, 1, 1], own_sem)
    own.start()
    fetch = pltpu.make_async_copy(token_ids, ids, ids_sem)
    fetch.start()
    load = pltpu.make_async_copy(head, weights, head_sem)
    load.start()

    barrier = pltpu.get_barrier_semaphore()
    for axis in range(3):
        for step in (1, -1, 2):
            pl.semaphore_signal(barrier, inc=1, device_id=neighbour(axis, step), device_id_type=MESH)
    pl.semaphore_signal(barrier, inc=1, device_id=sibling, device_id_type=MESH)
    pl.semaphore_wait(barrier, 10)
    own.wait()

    sent = {}

    def kind(group):
        return group % KINDS if group < LATE else KINDS + group - LATE

    def remote(src, dst, target, group):
        return pltpu.make_async_remote_copy(
            src_ref=src, dst_ref=dst, send_sem=send_sem.at[kind(group)], recv_sem=recv_sem.at[group],
            device_id=target, device_id_type=MESH)

    def move(r, src, dst, cols, target, group, side=0):
        a = at(r, *src)
        remote(blocks.at[(0,) + a + (slice(None), cols)],
               blocks.at[(side,) + at(r, *dst) + (slice(None), cols)], target, group).start()
        size = cols.size // UNIT
        for e in src:
            size *= e[1] if isinstance(e, tuple) else 1
        sent[group] = sent.get(group, 0) + size

    def arrived(group):
        where = blocks.at[region(sent[group])]
        remote(where, where, sibling, group).wait_recv()

    def drained():
        totals = {}
        for group, count in sent.items():
            totals[kind(group)] = totals.get(kind(group), 0) + count
        for k, count in totals.items():
            where = blocks.at[region(count)]
            pltpu.make_async_remote_copy(
                src_ref=where, dst_ref=where, send_sem=send_sem.at[k], recv_sem=recv_sem.at[0],
                device_id=sibling, device_id_type=MESH).wait_send()

    def cols_of(k, r):
        return pl.ds(START[k][r] * UNIT, STAGES[k][r] * UNIT)

    def ring(r, which, src, dst, cols, group, steps):
        for step in steps:
            to = list(dst)
            to[which] = (1 - step) % 4
            move(r, src, tuple(to), cols, neighbour(ROTATIONS[r][which], step), group)

    def live(k):
        return [r for r in RS if STAGES[k][r]]

    def second(k):
        for step in (1, -1) if k in PASSED else (1, -1, 2):
            for r in live(k):
                ring(r, 1, (ALL, 1, 1), (ALL, 1, 1), cols_of(k, r), k * KINDS + SECOND, (step,))

    def onward(k):
        arrived(k * KINDS + SECOND)
        for r in live(k):
            move(r, ((0, 2), 0, 1), ((0, 2), 3, 1), cols_of(k, r), neighbour(ROTATIONS[r][1], 1), k * KINDS + PASS)
            move(r, ((2, 2), 2, 1), ((2, 2), 3, 1), cols_of(k, r), neighbour(ROTATIONS[r][1], -1), k * KINDS + PASS)

    def third(k):
        arrived(k * KINDS + (PASS if k in PASSED else SECOND))
        for step in (1, -1, 2) if k in WHOLE else (1, -1):
            for r in live(k):
                ring(r, 2, (ALL, ALL, 1), (ALL, ALL, 1), cols_of(k, r), k * KINDS + DIRECT, (step,))

    def arrive(k):
        arrived(k * KINDS + DIRECT)
        for r in live(k):
            if k not in WHOLE:
                move(r, ((0, 2), ALL, 0), ((0, 2), ALL, 3), cols_of(k, r), neighbour(ROTATIONS[r][2], 1), k * KINDS + FORWARD)
                move(r, ((2, 2), ALL, 2), ((2, 2), ALL, 3), cols_of(k, r), neighbour(ROTATIONS[r][2], -1), k * KINDS + FORWARD)
        for r in live(k):
            part = ALL if k in WHOLE else NEAR
            move(r, (ALL, ALL, part), (ALL, ALL, part), cols_of(k, r), sibling, k * KINDS + SHARE, 1)

    def finish(k):
        arrived(k * KINDS + FORWARD)
        for r in live(k):
            move(r, (ALL, ALL, 3), (ALL, ALL, 3), cols_of(k, r), sibling, k * KINDS + SHARE_FAR, 1)

    def shared(k):
        arrived(k * KINDS + SHARE)
        if k not in WHOLE:
            arrived(k * KINDS + SHARE_FAR)

    half_lanes = logits.shape[1] // 2

    tops, tallies = {}, {}
    order = [(c, sz) for c in range(2) for sz in range(4)]

    def tally(side):
        top = jnp.broadcast_to(tops[side], (8, half_lanes))
        wanted = jnp.concatenate(
            [rolled[pl.ds(lax.rem(z + sz + 3, 4) * 2 + (1 - core if c else core), 1), :]
             for c, sz in order if c == side], axis=1)
        row = lax.broadcasted_iota(jnp.int32, (8, half_lanes), 0)
        offset = jnp.broadcast_to(wanted, (8, half_lanes)) - row
        total = picked = jnp.zeros((8, half_lanes), jnp.float32)
        for first in range(0, logits.shape[0], 8):
            v = logits[pl.ds(first, 8), pl.ds(side * half_lanes, half_lanes)]
            total = total + jnp.exp(v - top)
            picked = picked + jnp.where(offset == first, v, 0.0)
        return jnp.sum(total, axis=0, keepdims=True), jnp.sum(picked, axis=0, keepdims=True)

    def multiply(side, k):
        cols = [cols_of(k, r) for r in live(k)]
        a = jnp.concatenate([weights[:, c] for c in cols], axis=1)
        b = jnp.concatenate([blocks[side, :, :, :, :, c].reshape(half_lanes, c.size) for c in cols], axis=1)
        product = lax.dot_general(a, b, (((1,), (1,)), ((), ())), preferred_element_type=jnp.float32)
        where = (pl.ds(0, vocab), pl.ds(side * half_lanes, half_lanes))
        if k == 0:
            logits[where] = product
        else:
            product = logits[where] + product
            logits[where] = product
        if k == FINAL[side]:
            tops[side] = jnp.max(product, axis=0, keepdims=True)

    for step in (1, -1, 2):
        for r in RS:
            ring(r, 0, (1, 1, 1), (1, 1, 1), cols_of(0, r), ONE, (step,))
    for step in (1, -1, 2):
        for r in RS:
            rest = pl.ds(START[1][r] * UNIT, (TOTAL[r] - STAGES[0][r]) * UNIT)
            ring(r, 0, (1, 1, 1), (1, 1, 1), rest, ONE_REST, (step,))

    logits[pl.ds(vocab, 4), :] = jnp.full((4, logits.shape[1]), -jnp.inf, jnp.float32)
    fetch.wait()
    lane = lax.broadcasted_iota(jnp.int32, (8, 128), 1)
    y0, x0 = lax.rem(y + 3, 4), lax.rem(x + 3, 4)
    turned = pltpu.roll(ids[...], lax.rem(128 - y0 * 32, 128), 1)
    near = pltpu.roll(turned, lax.rem(128 - x0 * 8, 128), 1)
    far = pltpu.roll(turned, lax.rem(160 - x0 * 8, 128), 1)
    turned = jnp.where(lax.rem(lane, 32) + x0 * 8 < 32, near, far) - (replica * 16 + tp) * vocab
    rolled[...] = jnp.where((turned >= 0) & (turned < vocab), turned, -1)

    def other(k):
        shared(k)
        multiply(1, k)
        if k == FINAL[1]:
            tallies[0] = tally(0)

    def rest():
        arrived(ONE_REST)

    def loaded():
        load.wait()

    steps = {"S": second, "G": onward, "T": third, "A": arrive, "F": finish, "M": lambda k: multiply(0, k), "N": other}
    arrived(ONE)
    for step in ORDER:
        if step == "rest":
            arrived(ONE_REST)
        elif step == "load":
            load.wait()
        else:
            steps[step[0]](int(step[1:]))

    tallies[1] = tally(1)
    top, total, picked = [
        jnp.concatenate(both, axis=1)
        for both in ((tops[0], tops[1]), (tallies[0][0], tallies[1][0]), (tallies[0][1], tallies[1][1]))]

    for k in range(8):
        part = slice(128 * k, 128 * k + 128)
        chip[k, 0:1, :] = top[:, part]
        chip[k, 1:2, :] = total[:, part]
        chip[k, 2:3, :] = picked[:, part]
    for k, (c, sz) in enumerate(order):
        dz = (sz - 1) % 4
        if c or dz:
            remote(chip.at[k], chip_in.at[c * 4 + (-dz) % 4], device(dz, 0, 0, c), CHIP).start()
    remote(chip_in.at[pl.ds(1, 7)], chip_in.at[pl.ds(1, 7)], sibling, CHIP).wait_recv()

    def merge(parts):
        best = functools.reduce(jnp.maximum, [p[0] for p in parts])
        total = sum(p[1] * jnp.exp(p[0] - best) for p in parts)
        return best, total, sum(p[2] for p in parts)

    def three_rows(ref, *at):
        return tuple(ref[at + (pl.ds(k, 1), slice(None))] for k in range(3))

    best, total, picked = merge([three_rows(chip, 1)] + [three_rows(chip_in, k) for k in range(1, 8)])
    plane[0:1, :] = best
    plane[1:2, :] = total
    plane[2:3, :] = picked
    for dy in range(4):
        for dx in range(4):
            if dy or dx:
                remote(plane, plane_in.at[(-dy) % 4 * 4 + (-dx) % 4], device(0, dy, dx, False), PLANE).start()
    remote(plane_in.at[pl.ds(1, 15)], plane_in.at[pl.ds(1, 15)], sibling, PLANE).wait_recv()
    group = lax.broadcasted_iota(jnp.int32, (1, 128), 1) // 8
    for sy in range(4):
        for sx in range(4):
            if sy or sx:
                mine = group == (1 - sy) % 4 * 4 + (1 - sx) % 4
                b, t, p = three_rows(plane_in, sy * 4 + sx)
                best, total, picked = jnp.where(mine, b, best), jnp.where(mine, t, total), jnp.where(mine, p, picked)
    final = best
    for shift in (8, 16, 32, 64):
        final = jnp.maximum(final, pltpu.roll(final, shift, 1))
    total = total * jnp.exp(best - final)
    for shift in (8, 16, 32, 64):
        total = total + pltpu.roll(total, shift, 1)
        picked = picked + pltpu.roll(picked, shift, 1)
    out[...] = (picked - final - jnp.log(total))[:, :8]

    drained()
    remote(chip_in.at[pl.ds(1, 7)], chip_in.at[pl.ds(1, 7)], sibling, CHIP).wait_send()
    remote(plane_in.at[pl.ds(1, 15)], plane_in.at[pl.ds(1, 15)], sibling, PLANE).wait_send()


def shards(hidden, head, token_ids):
    vocab, depth = head.shape
    lanes = token_ids.shape[0]
    out = pl.pallas_call(
        kernel,
        out_shape=jax.ShapeDtypeStruct((1, 8), jnp.float32),
        in_specs=[pl.BlockSpec(memory_space=pl.ANY)] * 3,
        out_specs=pl.BlockSpec(memory_space=pltpu.VMEM),
        scratch_shapes=[
            pltpu.VMEM((2, 4, 4, 4, 8, depth), jnp.bfloat16),
            pltpu.VMEM((vocab, depth), jnp.bfloat16),
            pltpu.VMEM((vocab + 4, lanes), jnp.float32),
            pltpu.VMEM((8, 128), jnp.int32),
            pltpu.VMEM((8, 128), jnp.int32),
            pltpu.VMEM((8, 8, 128), jnp.float32),
            pltpu.VMEM((8, 8, 128), jnp.float32),
            pltpu.VMEM((8, 128), jnp.float32),
            pltpu.VMEM((16, 8, 128), jnp.float32),
            pltpu.SemaphoreType.DMA,
            pltpu.SemaphoreType.DMA,
            pltpu.SemaphoreType.DMA,
            pltpu.SemaphoreType.DMA((KINDS + 4,)),
            pltpu.SemaphoreType.DMA((LATE + 4,)),
        ],
        compiler_params=pltpu.CompilerParams(
            collective_id=0, has_side_effects=True, vmem_limit_bytes=60 * 1024 * 1024),
        name="logprob",
    )(hidden, head, token_ids.reshape(8, 128))
    return out.reshape(8)


def solution(mesh):
    in_specs = (P(("replica", "tp"), None), P(("replica", "tp"), None), P())
    out_specs = P(("replica", "tp"))
    return jax.shard_map(shards, mesh=mesh, in_specs=in_specs, out_specs=out_specs, check_vma=False)
```

time: 149 us -> 63.6 us (0.43)
  waiting for transfers between devices: 87.5 us -> 0 us
  Pallas kernels: 0 us -> 62.3 us
  matrix products: 27.3 us -> 0 us
  blocking collectives: 16.8 us -> 0 us
  between operations: 13.5 us -> 0.01 us
  other arithmetic: 3.93 us -> 0 us
    all_gather x1 -> x0, waiting for transfers between devices: 86.8 us -> none  [shards(): gathered = lax.all_gather(hidden, ('replica', 'tp'), axis=0, tiled=True)]
    pallas_call x0 -> x1, Pallas kernels: none -> 62.3 us  [shards(): pl.pallas_call(kernel, out_shape=jax.ShapeDtypeStruct((1, 8), jnp.float32...]
    dot_general x1 -> x0, matrix products: 27.3 us -> none  [shards(): lax.dot_general(gathered, head, (((1,), (1,)), ((), ())), preferred_eleme...]
    all_to_all x1 -> x0, blocking collectives: 16.8 us -> none  [in_one_piece(): lax.all_to_all(both, axis, split_axis=split_dim, concat_axis=concat_dim,...]
    reduce_sum x2 -> x0, other arithmetic: 3.27 us -> none  [the longest x1 3.15 us: shards(): row_total = jnp.sum(jnp.exp(logits - row_top[:, None]), axis=1)]
  transfers between devices with their start and end apart: 1 -> 0, of which waited for: 1 -> 0; matrix products, arithmetic and copies ran while one was open for 0% -> 0% of each run, Pallas kernels for 0% -> 0%
where the time goes in v2:
time: 63.6 us; the launch traced here: 63.5 us
  Pallas kernels  62.3 us (98%)
  local copies, waits for them, and re-layouts  1.19 us (2%)
    pallas_call x1, Pallas kernels, shards(): pl.pallas_call(kernel, out_shape=jax.ShapeDtypeStruct((1, 8), jnp.float32...  62.3 us

profile of v2, /device:TPU:1, one launch (start us, length us, event | category | flops | bytes accessed | tf_op | source)
XLA Modules:
  0.0 63.5 jit_solution(15269201311032477619)
XLA Ops:
  0.0 62.3 %logprob.1 = f32[1,8]{1,0:T(1,128)} custom-call(bf16[8,8192]{1,0:T(8,128)(2,1)} %hidden.1, bf16[1188,8192]{1,0:T(8,128)(2,1)} %head.1, s32[8,128]{1,0:T(8,128)} %bitcast.2), custom_call_target="tpu_custom_call" | custom-call | tf_op jit(solution)/shard_map/logprob/pallas_call | solution.py:299
  62.3 1.2 %copy.5 = f32[8]{0:T(128)} copy(f32[8]{0:T(128)} %bitcast.3) | data formatting | bytes 64

commit v3 on v2

--- a/solution.py
+++ b/solution.py
@@ -130,8 +130,8 @@
         return [r for r in RS if STAGES[k][r]]
 
     def second(k):
-        for step in (1, -1) if k in PASSED else (1, -1, 2):
-            for r in live(k):
+        for r in live(k):
+            for step in (1, -1) if k in PASSED else (1, -1, 2):
                 ring(r, 1, (ALL, 1, 1), (ALL, 1, 1), cols_of(k, r), k * KINDS + SECOND, (step,))
 
     def onward(k):
@@ -142,8 +142,8 @@
 
     def third(k):
         arrived(k * KINDS + (PASS if k in PASSED else SECOND))
-        for step in (1, -1, 2) if k in WHOLE else (1, -1):
-            for r in live(k):
+        for r in live(k):
+            for step in (1, -1, 2) if k in WHOLE else (1, -1):
                 ring(r, 2, (ALL, ALL, 1), (ALL, ALL, 1), cols_of(k, r), k * KINDS + DIRECT, (step,))
 
     def arrive(k):

time: 63.6 us -> 63.6 us (level)
  no operation moved by 1% of the time
where the time goes in v3:
time: 63.6 us; the launch traced here: 63.5 us
  Pallas kernels  62.2 us (98%)
  local copies, waits for them, and re-layouts  1.19 us (2%)
    pallas_call x1, Pallas kernels, shards(): pl.pallas_call(kernel, out_shape=jax.ShapeDtypeStruct((1, 8), jnp.float32...  62.2 us

profile of v3, /device:TPU:1, one launch (start us, length us, event | category | flops | bytes accessed | tf_op | source)
XLA Modules:
  0.0 63.5 jit_solution(567276503021999198)
XLA Ops:
  0.0 62.2 %logprob.1 = f32[1,8]{1,0:T(1,128)} custom-call(bf16[8,8192]{1,0:T(8,128)(2,1)} %hidden.1, bf16[1188,8192]{1,0:T(8,128)(2,1)} %head.1, s32[8,128]{1,0:T(8,128)} %bitcast.2), custom_call_target="tpu_custom_call" | custom-call | tf_op jit(solution)/shard_map/logprob/pallas_call | solution.py:299
  62.3 1.2 %copy.5 = f32[8]{0:T(128)} copy(f32[8]{0:T(128)} %bitcast.3) | data formatting | bytes 64
